TPU v7x, 32 devices: a whole 2x2x4 slice. The times are simulated.
32 devices in a mesh: groups: 2 (over y), seq: 4 (over z), batch: 2 (over x), head: 2 (over core).
Axes of the slice: x: 2, y: 2, z: 4, core: 2. Of those that a mesh axis runs over, the one named last changes fastest.
Arguments:
- hidden_in: bfloat16 [64, 4096], P(('groups', 'batch'), 'seq'), parts along dimension 0, may hold values from -400 to 400
- norm_gain_vector: bfloat16 [4096], P('seq'), may hold values from 0.099609375 to 1.8984375
- w_query: bfloat16 [4096, 4096], P('seq', 'head'), may hold values from -0.09375 to 0.09375
- key_cache_rows: bfloat16 [64, 4096, 128], P(('groups', 'batch'), 'seq'), parts along dimension 0, may hold values from -360 to 360
- value_cache_rows: bfloat16 [64, 4096, 128], P(('groups', 'batch'), 'seq'), parts along dimension 0, may hold values from -6 to 6
- k_new: bfloat16 [64, 128], P(('groups', 'batch')), parts along dimension 0, may hold values from -360 to 360
- v_new: bfloat16 [64, 128], P(('groups', 'batch')), parts along dimension 0, may hold values from -6 to 6
- lengths: int32 [64], P(('groups', 'batch')), parts along dimension 0, may hold values from 1 to 4096, as said below
- w_out: bfloat16 [4096, 4096], P('head', 'seq'), may hold values from -0.09375 to 0.09375
Outputs:
- layer_out: float32 [64, 4096], P(('groups', 'batch'), ('seq', 'head')), parts along dimension 0
There are 2 independent parts, one for each index of `groups`. A program takes and returns all parts, laid end to end along the dimension named above; an argument that names none is the same for every part. Nothing has to cross between parts.
Inputs may be any that keep to these rules, and one draw needn't show every extreme that they name: `lengths`: every sequence has at least one cached position; some sequence of each draw uses all 4096.
All inputs are finite; a program needn't handle non-finite values.
Results may differ from a plain program's by a relative error of at most 0.008.
Values sent between devices are 32-bit elements; how exact they have to be, the bound alone decides.
A program may use at most 64 MiB of HBM per device.

v0:
```python
import jax
import jax.numpy as jnp
from jax import lax
from jax.sharding import PartitionSpec as P

D = 4096
HD = 128


def combined_all(value, axis, join):
    pieces = jax.tree.map(lambda part: lax.all_gather(part, axis), value)
    head = jax.tree.map(lambda part: part[0], pieces)
    tail = jax.tree.map(lambda part: part[1:], pieces)
    total, _ = lax.scan(lambda total, share: (join(total, share), None), head, tail)
    return total


def combine(earlier, later):
    top_a, total_a, summed_a = earlier
    top_b, total_b, summed_b = later
    top = jnp.maximum(top_a, top_b)
    factor_a = jnp.exp(top_a - top)
    factor_b = jnp.exp(top_b - top)
    return (
        top,
        total_a * factor_a + total_b * factor_b,
        summed_a * factor_a[..., None] + summed_b * factor_b[..., None],
    )


def shards(
    hidden_in,
    norm_gain_vector,
    w_query,
    key_cache_rows,
    value_cache_rows,
    k_new,
    v_new,
    lengths,
    w_out,
):
    inputs = hidden_in.astype(jnp.float32)
    squares = lax.psum(jnp.sum(inputs * inputs, axis=-1), "seq")
    inv_rms = lax.rsqrt(squares / D + 1e-05)
    normed = (inputs * inv_rms[:, None] * norm_gain_vector.astype(jnp.float32)[None, :]).astype(
        jnp.bfloat16
    )
    partial_query = jnp.dot(normed, w_query, preferred_element_type=jnp.float32)
    inverse_root_norm = 1.0 / HD**0.5
    query_vectors = (lax.psum(partial_query, "seq") * inverse_root_norm).astype(jnp.bfloat16)
    seq_rows = query_vectors.shape[0]
    query_vectors = query_vectors.reshape(seq_rows, query_vectors.shape[1] // HD, HD)
    block_len = key_cache_rows.shape[1]
    scores = jnp.einsum(
        "irm,iam->ira", query_vectors, key_cache_rows, preferred_element_type=jnp.float32
    )
    own = jnp.einsum("bhd,bd->bh", query_vectors, k_new, preferred_element_type=jnp.float32)
    positions = lax.axis_index("seq") * block_len + lax.iota(jnp.int32, block_len)
    live_mask = (positions[None, :] < lengths[:, None])[:, None, :]
    local_top = jnp.maximum(jnp.max(jnp.where(live_mask, scores, -jnp.inf), axis=-1), own)
    softmax_weights = jnp.where(live_mask, jnp.exp(scores - local_top[..., None]), jnp.float32(0.0))
    local_total = jnp.sum(softmax_weights, axis=-1)
    local_partial_sum = jnp.einsum(
        "ajq,aqe->aje",
        softmax_weights.astype(jnp.bfloat16),
        value_cache_rows,
        preferred_element_type=jnp.float32,
    )
    top, totals, summed = combined_all((local_top, local_total, local_partial_sum), "seq", combine)
    fresh = jnp.exp(own - top)
    totals = totals + fresh
    result = (summed + fresh[..., None] * v_new.astype(jnp.float32)[:, None, :]) / totals[..., None]
    attended = result.astype(jnp.bfloat16).reshape(seq_rows, -1)
    partial_out = jnp.dot(attended, w_out, preferred_element_type=jnp.float32)
    return lax.psum_scatter(partial_out, "head", scatter_dimension=1, tiled=True)


def solution(mesh):
    placed = (
        P(("groups", "batch"), "seq"),
        P("seq"),
        P("seq", "head"),
        P(("groups", "batch"), "seq", None),
        P(("groups", "batch"), "seq", None),
        P(("groups", "batch"), None),
        P(("groups", "batch"), None),
        P(("groups", "batch")),
        P("head", "seq"),
    )
    return jax.shard_map(
        shards,
        mesh=mesh,
        in_specs=placed,
        out_specs=P(("groups", "batch"), ("seq", "head")),
        check_vma=False,
    )
```

profile of v0, /device:TPU:0, one launch (start us, length us, event | category | flops | bytes accessed | tf_op | source)
XLA Modules:
  0.0 123.9 jit_solution(10203687832632314913)
XLA Ops:
  6.5 0.0 copy-start
  6.5 0.0 copy-start.2
  6.5 0.0 copy-start.3
  6.5 0.0 all-reduce.2.cloned.1.call-start
  6.5 0.9 fusion.10
  7.5 13.5 %psum.14 = f32[16]{0:T(128)S(1)} all-reduce(f32[16]{0:T(128)S(1)} %fusion.10), channel_id=1, replica_groups=mesh['groups'=2,'seq'=4,'batch'=2,'head'=2] {'seq'}, use_global_device_ids=true, to_apply=%region_1.0 | all-reduce | flops 16 | bytes 128 | tf_op jit(solution)/shard_map/psum | solution.py:43
  20.9 0.7 convert_element_type.22
  21.6 3.6 %fusion.17 = f32[16,2048]{1,0:T(8,128)} fusion(bf16[1024,2048]{1,0:T(8,128)(2,1)} %param.13, bf16[16,1024]{1,0:T(8,128)(2,1)} %param.11, f32[1024]{0:T(1024)S(1)} %convert_element_type.22, f32[16]{0:T(128)S(1)} %add_rsqrt_fusion), kind=kOutput, calls=%fused_computation.27 | convolution fusion | flops 67174400 | bytes 4362304 | tf_op jit(solution)/shard_map/dot_general | solution.py:48
  25.2 0.0 all-reduce.2.cloned.1.call-update
  25.2 0.0 reduce-scatter.2.cloned.1.call-start
  25.3 0.0 copy-done.2
  25.3 0.0 copy-done.3
  25.3 0.1 broadcast_compare_fusion
  25.4 32.8 %all-reduce.2.cloned.1.call-done = f32[16,2048]{1,0:T(8,128)} async-done(((f32[16,2048]{1,0:T(8,128)}), f32[16,2048]{1,0:T(8,128)}) %all-reduce.2.cloned.1.call-update) | async-done | bytes 131088 | tf_op jit(solution)/shard_map/psum | solution.py:50
  58.3 0.0 copy-start.1
  58.3 1.1 fusion.13
  59.3 0.0 copy-done
  59.4 0.1 fusion.21
  59.5 3.5 %select_reduce_fusion = (f32[16,16]{1,0:T(8,128)S(1)}, f32[16,16,1024]{2,1,0:T(8,128)S(1)}) fusion(pred[16,1024]{1,0:T(8,128)(4,1)S(1)} %broadcast_compare_fusion, bf16[16,16,128]{2,1,0:T(8,128)(2,1)S(1)} %bitcast.42, bf16[16,1024,128]{2,1,0:T(8,128)(2,1)} %param.14), kind=kOutput, calls=%fused_computation.9 | convolution fusion | flops 67632896 | bytes 5325824 | tf_op jit(solution)/shard_map/irm,iam->ira/dot_general | solution.py:54
  63.0 13.1 %all-gather = f32[64,16]{1,0:T(8,128)S(1)} all-gather(f32[16,16]{1,0:T(8,128)S(1)} %max.6), channel_id=2, replica_groups=mesh['groups'=2,'seq'=4,'batch'=2,'head'=2] {'seq'}, dimensions={0}, use_global_device_ids=true | all-gather | bytes 5120 | tf_op jit(solution)/shard_map/all_gather | solution.py:11
  76.2 0.3 fusion.4
  76.5 13.2 %all-gather.1 = f32[64,16]{1,0:T(8,128)S(1)} all-gather(f32[16,16]{1,0:T(8,128)S(1)} %fusion.4), channel_id=3, replica_groups=mesh['groups'=2,'seq'=4,'batch'=2,'head'=2] {'seq'}, dimensions={0}, use_global_device_ids=true | all-gather | bytes 5120 | tf_op jit(solution)/shard_map/all_gather | solution.py:11
  89.8 0.0 copy-done.1
  89.8 0.8 fusion.5
  90.5 14.7 %all-gather.2 = f32[64,16,128]{2,1,0:T(8,128)S(1)} all-gather(f32[16,16,128]{2,1,0:T(8,128)S(1)} %fusion.5), channel_id=4, replica_groups=mesh['groups'=2,'seq'=4,'batch'=2,'head'=2] {'seq'}, dimensions={0}, use_global_device_ids=true | all-gather | bytes 655360 | tf_op jit(solution)/shard_map/all_gather | solution.py:11
  105.2 0.6 while.14
  105.3 0.2 fusion.35
  105.5 0.2 fusion.35
  105.7 0.2 fusion.35
  105.9 0.1 divide_convert_fusion
  106.0 3.5 %fusion.14 = f32[16,1024]{1,0:T(8,128)} fusion(bf16[2048,1024]{1,0:T(8,128)(2,1)} %param.19, bf16[2,8,16,128]{3,2,1,0:T(8,128)(2,1)S(1)} %bitcast.40), kind=kOutput, calls=%fused_computation.24 | convolution fusion | flops 67108864 | bytes 4325376 | tf_op jit(solution)/shard_map/dot_general | solution.py:74
  109.5 0.0 reduce-scatter.2.cloned.1.call-update
  109.5 7.6 %reduce-scatter.2.cloned.1.call-done = f32[16,512]{1,0:T(8,128)} async-done(((f32[16,1024]{1,0:T(8,128)}), f32[16,512]{1,0:T(8,128)}) %reduce-scatter.2.cloned.1.call-update) | async-done | bytes 32784 | tf_op jit(solution)/shard_map/reduce_scatter | solution.py:75
  (15 shorter events, 0.1 us)
Async XLA Ops:
  6.5 52.8 %copy-start = (bf16[16,128]{1,0:T(8,128)(2,1)S(1)}, bf16[16,128]{1,0:T(8,128)(2,1)}, u32[]{:S(2)}) copy-start(bf16[16,128]{1,0:T(8,128)(2,1)} %param.16) | copy-start | bytes 12292
  6.5 18.8 %copy-start.2 = (bf16[16,128]{1,0:T(8,128)(2,1)S(1)}, bf16[16,128]{1,0:T(8,128)(2,1)}, u32[]{:S(2)}) copy-start(bf16[16,128]{1,0:T(8,128)(2,1)} %param.17) | copy-start | bytes 12292
  6.5 18.8 %copy-start.3 = (s32[16]{0:T(128)S(1)}, s32[16]{0:T(128)}, u32[]{:S(2)}) copy-start(s32[16]{0:T(128)} %param.18) | copy-start | bytes 196
  6.5 51.7 %all-reduce.2.cloned.1.call-start = ((), (), s32[]{:S(2)}) async-start(), calls=%async_computation.1 | async-start | bytes 262144 | tf_op jit(solution)/shard_map/psum | solution.py:50
  25.2 91.8 %reduce-scatter.2.cloned.1.call-start = ((), (), s32[]{:S(2)}) async-start(), calls=%async_computation.2 | async-start | bytes 98304 | tf_op jit(solution)/shard_map/reduce_scatter | solution.py:75
  58.3 31.5 %copy-start.1 = (bf16[16,1024,128]{2,1,0:T(8,128)(2,1)S(1)}, bf16[16,1024,128]{2,1,0:T(8,128)(2,1)}, u32[]{:S(2)}) copy-start(bf16[16,1024,128]{2,1,0:T(8,128)(2,1)} %param.15) | copy-start | bytes 12582916
Sparse Core Ops, SparseCore 0:
  25.3 32.8 all-reduce.1
  109.6 7.3 reduce-scatter.1
where the time goes:
time: 124 us
  blocking collectives  54.5 us (44%)
  waiting for transfers between devices  40.4 us (33%)
  between operations  13.5 us (11%)
  matrix products  11.5 us (9%)
  other arithmetic  3.82 us (3%)
    all_gather x3, blocking collectives, combined_all(): pieces = jax.tree.map(lambda part: lax.all_gather(part, axis), value)  41 us
    psum x1, waiting for transfers between devices, shards(): lax.psum(partial_query, 'seq') * inverse_root_norm  32.8 us
    psum x1, blocking collectives, shards(): squares = lax.psum(jnp.sum(inputs * inputs, axis=-1), 'seq')  13.5 us
    reduce_scatter x1, waiting for transfers between devices, shards(): lax.psum_scatter(partial_out, 'head', scatter_dimension=1, tiled=True)  7.55 us
    dot_general x1, matrix products, shards(): partial_query = jnp.dot(normed, w_query, preferred_element_type=jnp.float32)  3.56 us
    dot_general x1, matrix products, shards(): jnp.einsum('irm,iam->ira', query_vectors, key_cache_rows, preferred_eleme...  3.54 us
    dot_general x1, matrix products, shards(): partial_out = jnp.dot(attended, w_out, preferred_element_type=jnp.float32)  3.47 us
  transfers between devices with their start and end apart: 2, of which 2 were waited for; matrix products, arithmetic and copies ran while one was open for 0% of the time, Pallas kernels for 0%

commit v1 on v0

--- a/solution.py
+++ b/solution.py
@@ -47,7 +47,9 @@
     )
     partial_query = jnp.dot(normed, w_query, preferred_element_type=jnp.float32)
     inverse_root_norm = 1.0 / HD**0.5
-    query_vectors = (lax.psum(partial_query, "seq") * inverse_root_norm).astype(jnp.bfloat16)
+    query_vectors = (
+        jnp.sum(lax.all_gather(partial_query, "seq"), axis=0) * inverse_root_norm
+    ).astype(jnp.bfloat16)
     seq_rows = query_vectors.shape[0]
     query_vectors = query_vectors.reshape(seq_rows, query_vectors.shape[1] // HD, HD)
     block_len = key_cache_rows.shape[1]

time: 124 us -> 103 us (0.83)
  waiting for transfers between devices: 40.4 us -> 6.14 us
  blocking collectives: 54.5 us -> 69.5 us
    psum x1 -> x0, waiting for transfers between devices: 32.8 us -> none  [shards(): lax.psum(partial_query, 'seq') * inverse_root_norm]
    all_gather x0 -> x1, blocking collectives: none -> 14.8 us  [shards(): lax.all_gather(partial_query, 'seq')]
    reduce_scatter x1, waiting for transfers between devices: 7.55 us -> 6.13 us  [shards(): lax.psum_scatter(partial_out, 'head', scatter_dimension=1, tiled=True)]
  transfers between devices with their start and end apart: 2 -> 1, of which waited for: 2 -> 1; matrix products, arithmetic and copies ran while one was open for 0% -> 0% of each run, Pallas kernels for 0% -> 0%
where the time goes in v1:
time: 103 us
  blocking collectives  69.5 us (67%)
  between operations  13.5 us (13%)
  matrix products  10.9 us (11%)
  waiting for transfers between devices  6.14 us (6%)
  other arithmetic  2.79 us (3%)
    all_gather x3, blocking collectives, combined_all(): pieces = jax.tree.map(lambda part: lax.all_gather(part, axis), value)  41.3 us
    all_gather x1, blocking collectives, shards(): lax.all_gather(partial_query, 'seq')  14.8 us
    psum x1, blocking collectives, shards(): squares = lax.psum(jnp.sum(inputs * inputs, axis=-1), 'seq')  13.5 us
    reduce_scatter x1, waiting for transfers between devices, shards(): lax.psum_scatter(partial_out, 'head', scatter_dimension=1, tiled=True)  6.13 us
    dot_general x1, matrix products, shards(): jnp.einsum('irm,iam->ira', query_vectors, key_cache_rows, preferred_eleme...  3.63 us
    dot_general x1, matrix products, shards(): partial_out = jnp.dot(attended, w_out, preferred_element_type=jnp.float32)  3.47 us
    dot_general x1, matrix products, shards(): partial_query = jnp.dot(normed, w_query, preferred_element_type=jnp.float32)  2.9 us
  transfers between devices with their start and end apart: 1, of which 1 were waited for; matrix products, arithmetic and copies ran while one was open for 0% of the time, Pallas kernels for 0%

profile of v1, /device:TPU:0, one launch (start us, length us, event | category | flops | bytes accessed | tf_op | source)
XLA Modules:
  0.0 103.0 jit_solution(2800619958699315193)
XLA Ops:
  6.5 0.0 copy-start
  6.5 0.0 copy-start.3
  6.5 0.0 reduce-scatter.2.cloned.1.call-start
  6.5 0.9 fusion.10
  7.4 13.5 %psum.7 = f32[16]{0:T(128)S(1)} all-reduce(f32[16]{0:T(128)S(1)} %fusion.10), channel_id=1, replica_groups=mesh['groups'=2,'seq'=4,'batch'=2,'head'=2] {'seq'}, use_global_device_ids=true, to_apply=%region_1.0 | all-reduce | flops 16 | bytes 128 | tf_op jit(solution)/shard_map/psum | solution.py:43
  20.9 0.7 convert_element_type.26
  21.6 2.9 %fusion.17 = f32[16,2048]{1,0:T(8,128)S(1)} fusion(bf16[1024,2048]{1,0:T(8,128)(2,1)} %param.13, bf16[16,1024]{1,0:T(8,128)(2,1)} %param.11, f32[1024]{0:T(1024)S(1)} %convert_element_type.26, f32[16]{0:T(128)S(1)} %add_rsqrt_fusion), kind=kOutput, calls=%fused_computation.27 | convolution fusion | flops 67174400 | bytes 4362304 | tf_op jit(solution)/shard_map/dot_general | solution.py:48
  24.5 14.8 %all-gather = f32[64,2048]{1,0:T(8,128)S(1)} all-gather(f32[16,2048]{1,0:T(8,128)S(1)} %fusion.17), channel_id=2, replica_groups=mesh['groups'=2,'seq'=4,'batch'=2,'head'=2] {'seq'}, dimensions={0}, use_global_device_ids=true | all-gather | bytes 655360 | tf_op jit(solution)/shard_map/all_gather | solution.py:51
  39.3 0.0 copy-start.1
  39.4 0.0 copy-done.3
  39.4 0.1 broadcast_compare_fusion
  39.5 0.0 copy-done
  39.5 0.1 fusion.21
  39.6 3.6 %select_reduce_fusion = (f32[16,16]{1,0:T(8,128)S(1)}, f32[16,16,1024]{2,1,0:T(8,128)S(1)}) fusion(pred[16,1024]{1,0:T(8,128)(4,1)S(1)} %broadcast_compare_fusion, bf16[16,16,128]{2,1,0:T(8,128)(2,1)S(1)} %bitcast.44, bf16[16,1024,128]{2,1,0:T(8,128)(2,1)} %param.14), kind=kOutput, calls=%fused_computation.9 | convolution fusion | flops 67632896 | bytes 5325824 | tf_op jit(solution)/shard_map/irm,iam->ira/dot_general | solution.py:56
  43.3 0.0 copy-start.2
  43.3 13.3 %all-gather.1 = f32[64,16]{1,0:T(8,128)S(1)} all-gather(f32[16,16]{1,0:T(8,128)S(1)} %max.6), channel_id=3, replica_groups=mesh['groups'=2,'seq'=4,'batch'=2,'head'=2] {'seq'}, dimensions={0}, use_global_device_ids=true | all-gather | bytes 5120 | tf_op jit(solution)/shard_map/all_gather | solution.py:11
  56.6 0.3 fusion.4
  56.9 13.2 %all-gather.2 = f32[64,16]{1,0:T(8,128)S(1)} all-gather(f32[16,16]{1,0:T(8,128)S(1)} %fusion.4), channel_id=4, replica_groups=mesh['groups'=2,'seq'=4,'batch'=2,'head'=2] {'seq'}, dimensions={0}, use_global_device_ids=true | all-gather | bytes 5120 | tf_op jit(solution)/shard_map/all_gather | solution.py:11
  70.1 0.0 copy-done.1
  70.1 0.8 fusion.5
  70.9 14.8 %all-gather.3 = f32[64,16,128]{2,1,0:T(8,128)S(1)} all-gather(f32[16,16,128]{2,1,0:T(8,128)S(1)} %fusion.5), channel_id=5, replica_groups=mesh['groups'=2,'seq'=4,'batch'=2,'head'=2] {'seq'}, dimensions={0}, use_global_device_ids=true | all-gather | bytes 655360 | tf_op jit(solution)/shard_map/all_gather | solution.py:11
  85.7 0.0 copy-done.2
  85.7 0.6 while.14
  85.8 0.2 fusion.35
  86.0 0.2 fusion.35
  86.2 0.2 fusion.35
  86.4 0.1 divide_convert_fusion
  86.5 3.5 %fusion.14 = f32[16,1024]{1,0:T(8,128)} fusion(bf16[2048,1024]{1,0:T(8,128)(2,1)} %param.19, bf16[2,8,16,128]{3,2,1,0:T(8,128)(2,1)S(1)} %bitcast.42), kind=kOutput, calls=%fused_computation.24 | convolution fusion | flops 67108864 | bytes 4325376 | tf_op jit(solution)/shard_map/dot_general | solution.py:76
  90.0 0.0 reduce-scatter.2.cloned.1.call-update
  90.0 6.1 %reduce-scatter.2.cloned.1.call-done = f32[16,512]{1,0:T(8,128)} async-done(((f32[16,1024]{1,0:T(8,128)}), f32[16,512]{1,0:T(8,128)}) %reduce-scatter.2.cloned.1.call-update) | async-done | bytes 32784 | tf_op jit(solution)/shard_map/reduce_scatter | solution.py:77
  (17 shorter events, 0.2 us)
Async XLA Ops:
  6.5 32.9 %copy-start = (bf16[16,128]{1,0:T(8,128)(2,1)S(1)}, bf16[16,128]{1,0:T(8,128)(2,1)}, u32[]{:S(2)}) copy-start(bf16[16,128]{1,0:T(8,128)(2,1)} %param.16) | copy-start | bytes 12292
  6.5 32.8 %copy-start.3 = (s32[16]{0:T(128)S(1)}, s32[16]{0:T(128)}, u32[]{:S(2)}) copy-start(s32[16]{0:T(128)} %param.18) | copy-start | bytes 196
  6.5 89.6 %reduce-scatter.2.cloned.1.call-start = ((), (), s32[]{:S(2)}) async-start(), calls=%async_computation.1 | async-start | bytes 98304 | tf_op jit(solution)/shard_map/reduce_scatter | solution.py:77
  39.3 30.8 %copy-start.1 = (bf16[16,1024,128]{2,1,0:T(8,128)(2,1)S(1)}, bf16[16,1024,128]{2,1,0:T(8,128)(2,1)}, u32[]{:S(2)}) copy-start(bf16[16,1024,128]{2,1,0:T(8,128)(2,1)} %param.15) | copy-start | bytes 12582916
  43.3 42.5 %copy-start.2 = (bf16[16,128]{1,0:T(8,128)(2,1)S(1)}, bf16[16,128]{1,0:T(8,128)(2,1)}, u32[]{:S(2)}) copy-start(bf16[16,128]{1,0:T(8,128)(2,1)} %param.17) | copy-start | bytes 12292
Sparse Core Ops, SparseCore 0:
  90.2 5.9 reduce-scatter.1
